TPU v7x, 32 devices: a whole 2x2x4 slice. The times are simulated.
32 devices in a mesh: blk: 16 (over z, x, core), rep: 2 (over y).
Axes of the slice: x: 2, y: 2, z: 4, core: 2. Of those that a mesh axis runs over, the one named last changes fastest.
Arguments:
- particles: bfloat16 [896, 2048], P(('blk', 'rep')), may hold values from -0.0029907227 to 0.0029907227
- scores: bfloat16 [896, 2048], P(('blk', 'rep')), may hold values from -60 to 60, as said below
- spread: float32 [1], replicated, may hold values from 0.00034816 to 0.00069632
Outputs:
- direction: float32 [896, 2048], P(('blk', 'rep'))
Inputs may be any that keep to these rules, and one draw needn't show every extreme that they name: `scores`: scores of the particles' log posterior.
All inputs are finite; a program needn't handle non-finite values.
Results may differ from a plain program's by a relative error of at most 0.0003.
Values may be sent and summed in bfloat16 or wider, within the bound.
A program may use at most 128 MiB of HBM per device.

v0:
```python
import jax
import jax.numpy as jnp
from jax import lax
from jax.sharding import PartitionSpec as P


def kernel_weights(targets, target_norm, source_x, inverse):
    cross_dots = lax.dot_general(
        targets, source_x, (((1,), (1,)), ((), ())), preferred_element_type=jnp.float32
    )
    source_wide = source_x.astype(jnp.float32)
    source_norm = jnp.sum(source_wide * source_wide, axis=1)
    squared = jnp.maximum(target_norm[:, None] + source_norm[None, :] - 2.0 * cross_dots, 0.0)
    return jnp.exp(-squared * inverse)


def shards(particles, scores, spread):
    inverse = 1.0 / spread[0]
    own_count = particles.shape[0]
    population = own_count * lax.axis_size("blk") * lax.axis_size("rep")
    targets = lax.all_gather(particles, "rep", axis=0, tiled=True)
    target_wide = targets.astype(jnp.float32)
    target_norm = jnp.sum(target_wide * target_wide, axis=1)
    stacked = jnp.stack([scores, particles], axis=0)
    source = lax.all_gather(stacked, "blk", axis=1, tiled=True)
    weights = kernel_weights(targets, target_norm, source[1], inverse)
    weights_low = weights.astype(jnp.bfloat16)
    combined_step = jnp.einsum(
        "ij,cjd->cid", weights_low, source, preferred_element_type=jnp.float32
    )
    row_total = jnp.sum(weights, axis=1)
    drive_sum = combined_step[0]
    pull_sum = combined_step[1]
    partial_value = (
        drive_sum + 2.0 * inverse * (target_wide * row_total[:, None] - pull_sum)
    ) / population
    return lax.psum_scatter(partial_value, "rep", scatter_dimension=0, tiled=True)


def solution(mesh):
    return jax.shard_map(
        shards,
        mesh=mesh,
        in_specs=(P(("blk", "rep"), None), P(("blk", "rep"), None), P()),
        out_specs=P(("blk", "rep"), None),
        check_vma=False,
    )
```

profile of v0, /device:TPU:0, one launch (start us, length us, event | category | flops | bytes accessed | tf_op | source)
XLA Modules:
  0.0 90.4 jit_solution(13617939061221818914)
XLA Ops:
  6.5 0.0 all-gather.3.cloned.1.call-start
  6.5 1.0 %pad_maximum_fusion = bf16[2,28,2048]{2,1,0:T(8,128)(2,1)S(1)} fusion(bf16[1,28,2048]{2,1,0:T(8,128)(2,1)} %bitcast.53, bf16[1,28,2048]{2,1,0:T(8,128)(2,1)} %bitcast.55), kind=kLoop, calls=%fused_computation.20 | loop fusion | flops 114688 | bytes 458752 | tf_op jit(solution)/shard_map/stack | solution.py:24
  7.5 0.9 %copy.6 = bf16[2,28,2048]{2,0,1:T(2,128)(2,1)} copy(bf16[2,28,2048]{2,1,0:T(8,128)(2,1)S(1)} %pad_maximum_fusion) | data formatting | bytes 458752 | tf_op jit(solution)/shard_map/stack | solution.py:24
  8.5 0.0 all-gather.3.cloned.1.call-update
  8.5 7.4 %all-gather = bf16[2,28,2048]{2,1,0:T(8,128)(2,1)S(1)} all-gather(bf16[1,28,2048]{2,1,0:T(8,128)(2,1)} %bitcast.54), channel_id=1, replica_groups=mesh['blk'=16,'rep'=2] {'rep'}, dimensions={0}, use_global_device_ids=true | all-gather | bytes 344064 | tf_op jit(solution)/shard_map/all_gather | solution.py:21
  15.9 0.1 reshape.6
  16.7 0.2 fusion.9
  16.8 43.2 %all-gather.3.cloned.1.call-done = bf16[2,448,2048]{2,0,1:T(2,128)(2,1)} async-done(((bf16[2,28,2048]{2,0,1:T(2,128)(2,1)}), bf16[2,448,2048]{2,0,1:T(2,128)(2,1)}) %all-gather.3.cloned.1.call-update) | async-done | bytes 3670032 | tf_op jit(solution)/shard_map/all_gather | solution.py:25
  60.0 3.6 %copy.8 = bf16[2,448,2048]{2,1,0:T(8,128)(2,1)S(1)} copy(bf16[2,448,2048]{2,0,1:T(2,128)(2,1)} %all-gather.3.cloned.1.call-done) | data formatting | bytes 7340032 | tf_op jit(solution)/shard_map/all_gather | solution.py:25
  63.7 0.0 copy-start
  63.7 0.4 multiply_reduce_fusion
  64.1 0.8 fusion.17
  64.9 0.8 copy-done
  65.7 0.0 copy-start.1
  65.7 1.2 %convolution_bitcast_fusion = f32[2,56,2048]{2,1,0:T(8,128)S(1)} fusion(bf16[56,448]{1,0:T(8,128)(2,1)S(1)} %get-tuple-element.6, bf16[2,448,2048]{2,0,1:T(2,128)(2,1)S(1)} %copy-done), kind=kOutput, calls=%fused_computation.1 | convolution fusion | flops 205520896 | bytes 4637696 | tf_op jit(solution)/shard_map/ij,cjd->cid/dot_general | solution.py:28
  67.0 0.2 fusion.13
  67.1 11.4 %fusion = f32[32,2048]{1,0:T(8,128)S(1)} fusion(f32[56,2048]{1,0:T(8,128)S(1)} %fusion.13), kind=kCustom, calls=%all-reduce-scatter | all-reduce-scatter fusion | flops 131073 | bytes 721408
  78.5 2.5 %collective-permute-start = (f32[4,2048]{1,0:T(4,128)S(1)}, f32[4,2048]{1,0:T(4,128)S(1)}, u32[]{:S(2)}, u32[]{:S(2)}) collective-permute-start(f32[4,2048]{1,0:T(4,128)S(1)} %slice.15), channel_id=1, source_target_pairs={{0,1},{2,3},{4,5},{6,7},{8,9},{10,11},{12,13},{14,15},{16,17},{18,... | collective-permute-start | bytes 98312
  81.0 0.0 copy-done.1
  81.0 0.6 dynamic-slice.4
  82.2 0.3 collective-permute-done
  82.6 0.2 concatenate
  82.8 0.7 constant_dynamic-slice_fusion
  (1 shorter events, 0.0 us)
Async XLA Ops:
  6.5 53.5 %all-gather.3.cloned.1.call-start = ((), (), s32[]{:S(2)}) async-start(), calls=%async_computation | async-start | bytes 3899392 | tf_op jit(solution)/shard_map/all_gather | solution.py:25
  63.7 2.0 %copy-start = (bf16[2,448,2048]{2,0,1:T(2,128)(2,1)S(1)}, bf16[2,448,2048]{2,0,1:T(2,128)(2,1)}, u32[]{:S(2)}) copy-start(bf16[2,448,2048]{2,0,1:T(2,128)(2,1)} %all-gather.3.cloned.1.call-done) | copy-start | bytes 11010052
  65.7 15.3 %copy-start.1 = (u32[32]{0:T(128)S(1)}, u32[32]{0:T(128)}, u32[]{:S(2)}) copy-start(u32[32]{0:T(128)} %constant.16) | copy-start | bytes 388
  78.5 4.0 %collective-permute-start = (f32[4,2048]{1,0:T(4,128)S(1)}, f32[4,2048]{1,0:T(4,128)S(1)}, u32[]{:S(2)}, u32[]{:S(2)}) collective-permute-start(f32[4,2048]{1,0:T(4,128)S(1)} %slice.15), channel_id=1, source_target_pairs={{0,1},{2,3},{4,5},{6,7},{8,9},{10,11},{12,13},{14,15},{16,17},{18,... | collective-permute-start | bytes 98312
Sparse Core Ops, SparseCore 0:
  9.6 50.3 all-gather.2
where the time goes:
time: 90.7 us; the launch traced here: 90.4 us
  waiting for transfers between devices  43.6 us (48%)
  blocking collectives  18.8 us (21%)
  between operations  14.8 us (16%)
  local copies, waits for them, and re-layouts  7.03 us (8%)
  starting transfers between devices  2.46 us (3%)
  matrix products  2.01 us (2%)
  other arithmetic  1.75 us (2%)
    all_gather x1, waiting for transfers between devices, shards(): source = lax.all_gather(stacked, 'blk', axis=1, tiled=True)  43.2 us
    unnamed x1, blocking collectives  11.4 us
    all_gather x1, blocking collectives, shards(): targets = lax.all_gather(particles, 'rep', axis=0, tiled=True)  7.42 us
    all_gather x1, local copies, waits for them, and re-layouts, shards(): source = lax.all_gather(stacked, 'blk', axis=1, tiled=True)  3.65 us
    unnamed x9, local copies, waits for them, and re-layouts  2.46 us
    unnamed x1, starting transfers between devices  2.46 us
  transfers between devices with their start and end apart: 2, of which 2 were waited for; matrix products, arithmetic and copies ran while one was open for 1% of the time, Pallas kernels for 0%

commit v1 on v0

--- a/solution.py
+++ b/solution.py
@@ -1,7 +1,16 @@
+import functools
 import jax
 import jax.numpy as jnp
 from jax import lax
 from jax.sharding import PartitionSpec as P
+
+
+def set_the_scenes(mine, comm_axis):
+    oldest = lax.all_gather(mine, comm_axis)
+    return jnp.concatenate(oldest, 1)
+
+
+pairs_all_supply_all = functools.partial(set_the_scenes, comm_axis="blk")
 
 
 def kernel_weights(targets, target_norm, source_x, inverse):
@@ -22,7 +31,7 @@
     target_wide = targets.astype(jnp.float32)
     target_norm = jnp.sum(target_wide * target_wide, axis=1)
     stacked = jnp.stack([scores, particles], axis=0)
-    source = lax.all_gather(stacked, "blk", axis=1, tiled=True)
+    source = pairs_all_supply_all(stacked)
     weights = kernel_weights(targets, target_norm, source[1], inverse)
     weights_low = weights.astype(jnp.bfloat16)
     combined_step = jnp.einsum(

time: 90.7 us -> 104 us (1.15)
  local copies, waits for them, and re-layouts: 7.03 us -> 12.9 us
  matrix products: 2.01 us -> 5.57 us
  waiting for transfers between devices: 43.6 us -> 46.4 us
    reshape x0 -> x1, local copies, waits for them, and re-layouts: none -> 5.61 us  [set_the_scenes(): return jnp.concatenate(oldest, 1)]
    all_gather x1, waiting for transfers between devices: 43.2 us -> 46 us  [set_the_scenes(): oldest = lax.all_gather(mine, comm_axis)]
    dot_general x1, matrix products: 1.25 us -> 3.3 us  [shards(): jnp.einsum('ij,cjd->cid', weights_low, source, preferred_element_type=jnp...]
    dot_general x1, matrix products: 0.76 us -> 2.27 us  [kernel_weights(): lax.dot_general(targets, source_x, (((1,), (1,)), ((), ())), preferred_el...]
    squeeze x0 -> x1, local copies, waits for them, and re-layouts: none -> 1.43 us  [shards(): weights = kernel_weights(targets, target_norm, source[1], inverse)]
    all_gather x1, local copies, waits for them, and re-layouts: 3.65 us -> 2.49 us  [set_the_scenes(): oldest = lax.all_gather(mine, comm_axis)]
where the time goes in v1:
time: 104 us; the launch traced here: 103 us
  waiting for transfers between devices  46.4 us (45%)
  blocking collectives  18.8 us (18%)
  between operations  14.8 us (14%)
  local copies, waits for them, and re-layouts  12.9 us (12%)
  matrix products  5.57 us (5%)
  other arithmetic  2.54 us (2%)
  starting transfers between devices  2.46 us (2%)
    all_gather x1, waiting for transfers between devices, set_the_scenes(): oldest = lax.all_gather(mine, comm_axis)  46 us
    unnamed x1, blocking collectives  11.4 us
    all_gather x1, blocking collectives, shards(): targets = lax.all_gather(particles, 'rep', axis=0, tiled=True)  7.42 us
    reshape x1, local copies, waits for them, and re-layouts, set_the_scenes(): return jnp.concatenate(oldest, 1)  5.61 us
    dot_general x1, matrix products, shards(): jnp.einsum('ij,cjd->cid', weights_low, source, preferred_element_type=jnp...  3.3 us
    unnamed x9, local copies, waits for them, and re-layouts  3.15 us
    all_gather x1, local copies, waits for them, and re-layouts, set_the_scenes(): oldest = lax.all_gather(mine, comm_axis)  2.49 us
    unnamed x1, starting transfers between devices  2.46 us
  transfers between devices with their start and end apart: 2, of which 2 were waited for; matrix products, arithmetic and copies ran while one was open for 1% of the time, Pallas kernels for 0%

profile of v1, /device:TPU:0, one launch (start us, length us, event | category | flops | bytes accessed | tf_op | source)
XLA Modules:
  0.0 103.5 jit_solution(4256327304731462741)
XLA Ops:
  6.5 0.0 all-gather.4.cloned.1.call-start
  6.5 1.7 %pad_maximum_fusion = bf16[2,28,2048]{2,1,0:T(8,128)(2,1)} fusion(bf16[1,28,2048]{2,1,0:T(8,128)(2,1)} %bitcast.45, bf16[1,28,2048]{2,1,0:T(8,128)(2,1)} %bitcast.47), kind=kLoop, calls=%fused_computation.21 | loop fusion | flops 114688 | bytes 458752 | tf_op jit(solution)/shard_map/stack | solution.py:33
  8.2 0.0 all-gather.4.cloned.1.call-update
  8.3 7.4 %all-gather.1 = bf16[2,28,2048]{2,1,0:T(8,128)(2,1)S(1)} all-gather(bf16[1,28,2048]{2,1,0:T(8,128)(2,1)} %bitcast.46), channel_id=1, replica_groups=mesh['blk'=16,'rep'=2] {'rep'}, dimensions={0}, use_global_device_ids=true | all-gather | bytes 344064 | tf_op jit(solution)/shard_map/all_gather | solution.py:30
  15.7 0.1 reshape.19
  16.4 0.2 fusion.12
  16.6 46.0 %all-gather.4.cloned.1.call-done = bf16[32,28,2048]{2,1,0:T(8,128)(2,1)} async-done(((bf16[2,28,2048]{2,1,0:T(8,128)(2,1)}), bf16[32,28,2048]{2,1,0:T(8,128)(2,1)}) %all-gather.4.cloned.1.call-update) | async-done | bytes 3670032 | tf_op jit(solution)/shard_map/all_gather | solution.py:9
  62.6 2.5 %copy.17 = bf16[16,2,28,2048]{3,2,0,1:T(8,128)(2,1)S(1)} copy(bf16[16,2,28,2048]{3,2,1,0:T(8,128)(2,1)} %bitcast.42) | data formatting | bytes 7340032 | tf_op jit(solution)/shard_map/all_gather | solution.py:9
  65.1 0.0 copy-start
  65.1 0.1 slice.13
  65.3 0.5 multiply_reduce_fusion
  65.8 1.5 %copy-done = bf16[32,28,2048]{2,1,0:T(8,128)(2,1)S(1)} copy-done((bf16[32,28,2048]{2,1,0:T(8,128)(2,1)S(1)}, bf16[32,28,2048]{2,1,0:T(8,128)(2,1)}, u32[]{:S(2)}) %copy-start) | copy-done | bytes 3670040
  67.3 5.6 %copy.9 = bf16[2,16,28,2048]{3,0,2,1:T(2,128)(2,1)} copy(bf16[2,16,28,2048]{3,2,0,1:T(8,128)(2,1)S(1)} %bitcast.43) | data formatting | bytes 7340032 | tf_op jit(solution)/shard_map/reshape | solution.py:10
  72.9 1.4 %squeeze.10 = bf16[448,2048]{1,0:T(8,128)(2,1)} reshape(bf16[1,16,28,2048]{3,2,1,0:T(8,128)(2,1)S(1)} %slice.13) | data formatting | bytes 3670016 | tf_op jit(solution)/shard_map/squeeze | solution.py:35
  74.4 0.1 add.21
  74.4 2.3 %fusion.19 = (f32[56]{0:T(128)S(1)}, bf16[56,448]{1,0:T(8,128)(2,1)S(1)}) fusion(f32[]{:T(128)} %bitcast.7, bf16[448,2048]{1,0:T(8,128)(2,1)} %squeeze.10, bf16[56,2048]{1,0:T(8,128)(2,1)S(1)} %reshape.19, f32[448]{0:T(512)S(1)} %add.21, f32[56]{0:T(128)S(1)} %fusion.12), kind=kOutput, calls=%fused_computation.25 | convolution fusion | flops 102961096 | bytes 2116804 | tf_op jit(solution)/shard_map/dot_general | solution.py:17
  76.7 0.0 copy-start.1
  76.7 3.3 %fusion.3 = f32[2,56,2048]{2,1,0:T(8,128)S(1)} fusion(bf16[2,448,2048]{2,0,1:T(2,128)(2,1)} %bitcast.44, bf16[56,448]{1,0:T(8,128)(2,1)S(1)} %get-tuple-element.6), kind=kOutput, calls=%fused_computation.4 | convolution fusion | flops 205520896 | bytes 4637696 | tf_op jit(solution)/shard_map/ij,cjd->cid/dot_general | solution.py:37
  80.0 0.2 fusion.16
  80.2 11.4 %fusion = f32[32,2048]{1,0:T(8,128)S(1)} fusion(f32[56,2048]{1,0:T(8,128)S(1)} %fusion.16), kind=kCustom, calls=%all-reduce-scatter | all-reduce-scatter fusion | flops 131073 | bytes 721408
  91.6 2.5 %collective-permute-start = (f32[4,2048]{1,0:T(4,128)S(1)}, f32[4,2048]{1,0:T(4,128)S(1)}, u32[]{:S(2)}, u32[]{:S(2)}) collective-permute-start(f32[4,2048]{1,0:T(4,128)S(1)} %slice.16), channel_id=1, source_target_pairs={{0,1},{2,3},{4,5},{6,7},{8,9},{10,11},{12,13},{14,15},{16,17},{18,... | collective-permute-start | bytes 98312
  94.1 0.0 copy-done.1
  94.1 0.6 dynamic-slice.4
  95.3 0.3 collective-permute-done
  95.6 0.2 concatenate
  95.9 0.7 constant_dynamic-slice_fusion
  (1 shorter events, 0.0 us)
Async XLA Ops:
  6.5 56.1 %all-gather.4.cloned.1.call-start = ((), (), s32[]{:S(2)}) async-start(), calls=%async_computation | async-start | bytes 4456448 | tf_op jit(solution)/shard_map/all_gather | solution.py:9
  65.1 2.2 %copy-start = (bf16[32,28,2048]{2,1,0:T(8,128)(2,1)S(1)}, bf16[32,28,2048]{2,1,0:T(8,128)(2,1)}, u32[]{:S(2)}) copy-start(bf16[32,28,2048]{2,1,0:T(8,128)(2,1)} %all-gather.4.cloned.1.call-done) | copy-start | bytes 11010052
  76.7 17.3 %copy-start.1 = (u32[32]{0:T(128)S(1)}, u32[32]{0:T(128)}, u32[]{:S(2)}) copy-start(u32[32]{0:T(128)} %constant.16) | copy-start | bytes 388
  91.6 4.0 %collective-permute-start = (f32[4,2048]{1,0:T(4,128)S(1)}, f32[4,2048]{1,0:T(4,128)S(1)}, u32[]{:S(2)}, u32[]{:S(2)}) collective-permute-start(f32[4,2048]{1,0:T(4,128)S(1)} %slice.16), channel_id=1, source_target_pairs={{0,1},{2,3},{4,5},{6,7},{8,9},{10,11},{12,13},{14,15},{16,17},{18,... | collective-permute-start | bytes 98312
Sparse Core Ops, SparseCore 0:
  9.5 53.0 all-gather.3
